TPU v7x, 32 devices: a whole 2x2x4 slice. The times are simulated.
32 devices in a mesh: group: 2 (over x), row: 4 (over y, core), col: 4 (over z).
Axes of the slice: x: 2, y: 2, z: 4, core: 2. Of those that a mesh axis runs over, the one named last changes fastest.
Arguments:
- pair_repr: bfloat16 [128, 128, 128], P(('group', 'row'), 'col'), may hold values from -6 to 6
- pair_mask: int32 [128, 128], P(('group', 'row'), 'col'), may hold values 0 or 1
- chain_id: int32 [128], replicated, may hold values from 0 to 7, never falling along the last dimension, each value on 1 to 32 neighbouring positions
- tri_in_gain: float32 [128], replicated, may hold values from 0.5 to 1.5
- tri_proj: bfloat16 [128, 512], replicated, may hold values from -0.5 to 0.5
- tri_gate: bfloat16 [128, 128], replicated, may hold values from -0.5 to 0.5
- tri_out_gain: float32 [128], replicated, may hold values from 0.5 to 1.5
- tri_out: bfloat16 [128, 128], replicated, may hold values from -0.5 to 0.5
- bias_gain: float32 [128], replicated, may hold values from 0.5 to 1.5
- bias_weight: bfloat16 [128, 16], replicated, may hold values from -0.5 to 0.5
- chain_bias: float32 [16], replicated, may hold values from -2 to 2
- tokens: bfloat16 [24, 128, 768], P(('group', 'row')), may hold values from -6 to 6
- noise_level: int32 [24], P(('group', 'row')), may hold values from 0 to 199
- attn_gain: float32 [768], replicated, may hold values from 0.5 to 1.5
- attn_weight: bfloat16 [4, 768, 768], P(None, None, 'col'), may hold values from -0.21875 to 0.21875
- out_weight: bfloat16 [768, 768], P('col'), may hold values from -0.21875 to 0.21875
- cotangent: bfloat16 [24, 128, 768], P(('group', 'row')), may hold values from -6 to 6
Outputs:
- pair_next: bfloat16 [128, 128, 128], P(('group', 'row'), 'col')
- pair_grad: float32 [128, 128, 128], P(('group', 'row'), 'col')
- bias_weight_grad: float32 [128, 16], replicated
- denoised: bfloat16 [24, 128, 768], P(('group', 'row'), 'col')
- token_grad: bfloat16 [24, 128, 768], P(('group', 'row'), 'col')
- attn_weight_grad: float32 [4, 768, 768], P(None, ('group', 'row'), 'col')
- out_weight_grad: float32 [768, 768], P('col', ('group', 'row'))
Inputs may be any that keep to these rules, and one draw needn't show every extreme that they name: `chain_id`: chain numbers never fall along the tokens.
All inputs are finite; a program needn't handle non-finite values. No bound on the sum of `pair_mask` on one device may be relied on, other than what follows from the above.
Results may differ from a plain program's by a relative error of at most 0.014.
Values may be sent and summed in bfloat16 or wider, within the bound.
No kernel may reach another device: no remote copies, remote signals or barrier semaphores. Data moves between devices by JAX's collectives and lax.ppermute only.
A program may use at most 64 MiB of HBM per device.

v0:
```python
import math
import jax
import jax.numpy as jnp
from jax import lax
from jax.sharding import PartitionSpec as P

LEVELS = 200
EPSILON = 1e-05
SIGMA_LOW = 0.1
SIGMA_SPAN = 100.0


def normalize(values):
    average = jnp.mean(values, -1, keepdims=True)
    centred = values - average
    return centred * lax.rsqrt(jnp.mean(centred * centred, -1, keepdims=True) + EPSILON)


def norm_back(gradient, values, norm_gain):
    average = jnp.mean(values, -1, keepdims=True)
    centred = values - average
    inverse = lax.rsqrt(jnp.mean(centred * centred, -1, keepdims=True) + EPSILON)
    normed = centred * inverse
    weighted = gradient * norm_gain
    return inverse * (
        weighted
        - jnp.mean(weighted, -1, keepdims=True)
        - normed * jnp.mean(weighted * normed, -1, keepdims=True)
    )


def noise_scale(levels):
    sigma_vals = SIGMA_LOW * SIGMA_SPAN ** (levels.astype(jnp.float32) / (LEVELS - 1))
    return lax.rsqrt(1.0 + sigma_vals * sigma_vals)


def shards(
    pair_repr,
    pair_mask,
    chain_id,
    tri_in_gain,
    tri_proj,
    tri_gate,
    tri_out_gain,
    tri_out,
    bias_gain,
    bias_weight,
    chain_bias,
    tokens,
    noise_level,
    attn_gain,
    attn_weight,
    out_weight,
    cotangent,
):
    rows_here = pair_repr.shape[0]
    cols_here = pair_repr.shape[1]
    channels = pair_repr.shape[2]
    token_count = chain_id.shape[0]
    heads_all = bias_weight.shape[1]
    hidden_width = attn_gain.shape[0]
    head_size = hidden_width // heads_all
    inverse_square_root = 1.0 / math.sqrt(head_size)
    row_index = lax.axis_index(("group", "row"))
    col_index = lax.axis_index("col")
    pair_tile = pair_repr.astype(jnp.float32)
    pair_in = (normalize(pair_tile) * tri_in_gain).astype(jnp.bfloat16)
    flat_in = pair_in.reshape(-1, channels)
    projected = jnp.dot(flat_in, tri_proj, preferred_element_type=jnp.float32).reshape(
        rows_here, cols_here, 4, channels
    )
    mask_tile = pair_mask.astype(jnp.float32)[:, :, None]
    left_proj = (jax.nn.sigmoid(projected[:, :, 0]) * projected[:, :, 1] * mask_tile).astype(
        jnp.bfloat16
    )
    right_proj = (jax.nn.sigmoid(projected[:, :, 2]) * projected[:, :, 3] * mask_tile).astype(
        jnp.bfloat16
    )
    gate_act = jax.nn.sigmoid(
        jnp.dot(flat_in, tri_gate, preferred_element_type=jnp.float32)
    ).reshape(rows_here, cols_here, channels)
    left_major = jnp.transpose(left_proj, (2, 0, 1))
    right_major = jnp.transpose(right_proj, (2, 0, 1))
    partial_rows = jnp.einsum(
        "cjk,cik->cji",
        lax.all_gather(right_major, ("group", "row"), axis=1, tiled=True),
        left_major,
        preferred_element_type=jnp.float32,
    )
    summed = lax.psum_scatter(partial_rows, "col", scatter_dimension=1, tiled=True)
    triangle = jnp.transpose(summed, (2, 1, 0))
    tri_normed = (normalize(triangle) * tri_out_gain).astype(jnp.bfloat16)
    update = jnp.dot(
        tri_normed.reshape(-1, channels), tri_out, preferred_element_type=jnp.float32
    ).reshape(rows_here, cols_here, channels)
    updated = pair_tile + gate_act * update
    bias_in = (normalize(updated) * bias_gain).astype(jnp.bfloat16)
    flat_bias = bias_in.reshape(-1, channels)
    bias_tile = jnp.dot(flat_bias, bias_weight, preferred_element_type=jnp.float32).reshape(
        rows_here, cols_here, heads_all
    )
    row_chain = lax.dynamic_slice_in_dim(chain_id, row_index * rows_here, rows_here)
    col_chain = lax.dynamic_slice_in_dim(chain_id, col_index * cols_here, cols_here)
    same_chain = (row_chain[:, None] == col_chain[None, :]).astype(jnp.float32)
    bias_tile = bias_tile + same_chain[:, :, None] * chain_bias
    bias_major = jnp.transpose(bias_tile.astype(jnp.bfloat16), (2, 0, 1))
    head_rows = lax.all_to_all(bias_major, "col", split_axis=0, concat_axis=2, tiled=True)
    per_head_bias = lax.all_gather(head_rows, ("group", "row"), axis=1, tiled=True).astype(
        jnp.float32
    )
    local_heads = per_head_bias.shape[0]
    scales = noise_scale(noise_level)

    def one_copy(carried, inputs):
        bias_sums, weight_sums, output_sums = carried
        token_rows, cot_rows, scaling = inputs
        sequence_length = token_rows.shape[0]
        scaled = scaling * token_rows.astype(jnp.float32)
        hidden = (normalize(scaled) * attn_gain).astype(jnp.bfloat16)
        projections = jnp.einsum(
            "nd,gde->gne", hidden, attn_weight, preferred_element_type=jnp.float32
        )
        query_rows = (
            projections[0].astype(jnp.bfloat16).reshape(sequence_length, local_heads, head_size)
        )
        key_matrix = (
            projections[1].astype(jnp.bfloat16).reshape(sequence_length, local_heads, head_size)
        )
        value_rows = (
            projections[2].astype(jnp.bfloat16).reshape(sequence_length, local_heads, head_size)
        )
        gate_sig = jax.nn.sigmoid(projections[3])
        logit_scores = (
            jnp.einsum("fuc,suc->ufs", query_rows, key_matrix, preferred_element_type=jnp.float32)
            * inverse_square_root
            + per_head_bias
        )
        exponent = jnp.exp(logit_scores)
        attention = exponent / jnp.sum(exponent, -1, keepdims=True)
        attention_probs = attention.astype(jnp.bfloat16)
        attended_rows = jnp.einsum(
            "vkq,qvy->kvy", attention_probs, value_rows, preferred_element_type=jnp.float32
        ).reshape(sequence_length, -1)
        gated_out = (gate_sig * attended_rows).astype(jnp.bfloat16)
        grad_gated = jnp.dot(cot_rows, out_weight.T, preferred_element_type=jnp.float32)
        grad_gate = grad_gated * attended_rows * gate_sig * (1.0 - gate_sig)
        attended_gradient = (
            (grad_gated * gate_sig)
            .astype(jnp.bfloat16)
            .reshape(sequence_length, local_heads, head_size)
        )
        probability_gradient = jnp.einsum(
            "fuc,suc->ufs", attended_gradient, value_rows, preferred_element_type=jnp.float32
        )
        value_gradient = jnp.einsum(
            "avj,vat->jat", attention_probs, attended_gradient, preferred_element_type=jnp.float32
        )
        grad_score = attention * (
            probability_gradient - jnp.sum(attention * probability_gradient, -1, keepdims=True)
        )
        score_gradient = grad_score.astype(jnp.bfloat16)
        query_gradient = (
            jnp.einsum(
                "vkq,qvy->kvy", score_gradient, key_matrix, preferred_element_type=jnp.float32
            )
            * inverse_square_root
        )
        key_gradient = (
            jnp.einsum(
                "avj,vat->jat", score_gradient, query_rows, preferred_element_type=jnp.float32
            )
            * inverse_square_root
        )
        grads = jnp.stack(
            [
                query_gradient.reshape(sequence_length, -1),
                key_gradient.reshape(sequence_length, -1),
                value_gradient.reshape(sequence_length, -1),
                grad_gate,
            ]
        ).astype(jnp.bfloat16)
        weight_sums = weight_sums + jnp.einsum(
            "nd,gne->gde", hidden, grads, preferred_element_type=jnp.float32
        )
        output_sums = output_sums + jnp.dot(
            gated_out.T, cot_rows, preferred_element_type=jnp.float32
        )
        return ((bias_sums + grad_score, weight_sums, output_sums), (gated_out, grads))

    start_sums = (
        jnp.zeros((local_heads, token_count, token_count), jnp.float32),
        jnp.zeros(attn_weight.shape, jnp.float32),
        jnp.zeros(out_weight.shape, jnp.float32),
    )
    final_sums, stacked = lax.scan(one_copy, start_sums, (tokens, cotangent, scales))
    bias_sums, weight_sums, output_sums = final_sums
    gated_all, grads_all = stacked
    token_share = token_count // lax.axis_size("col")
    attn_parts = jnp.einsum(
        "tnd,de->tne", gated_all, out_weight, preferred_element_type=jnp.float32
    )
    hidden_parts = jnp.einsum(
        "tgne,gde->tnd", grads_all, attn_weight, preferred_element_type=jnp.float32
    )
    attn_out, grad_hidden = (
        lax.psum_scatter(attn_parts, "col", scatter_dimension=1, tiled=True),
        lax.psum_scatter(hidden_parts, "col", scatter_dimension=1, tiled=True),
    )
    first_token = col_index * token_share
    token_mine = lax.dynamic_slice_in_dim(tokens, first_token, token_share, 1)
    cot_mine = lax.dynamic_slice_in_dim(cotangent, first_token, token_share, 1)
    scaled_mine = scales[:, None, None] * token_mine.astype(jnp.float32)
    denoised = (scaled_mine + attn_out).astype(jnp.bfloat16)
    grad_scaled = cot_mine.astype(jnp.float32) + norm_back(grad_hidden, scaled_mine, attn_gain)
    token_grad = (scales[:, None, None] * grad_scaled).astype(jnp.bfloat16)
    bias_rows_sum, out_grad, weight_grad = (
        lax.psum_scatter(bias_sums, ("group", "row"), scatter_dimension=1, tiled=True),
        lax.psum_scatter(output_sums, ("group", "row"), scatter_dimension=1, tiled=True),
        lax.psum_scatter(weight_sums, ("group", "row"), scatter_dimension=1, tiled=True),
    )
    bias_back = lax.all_to_all(bias_rows_sum, "col", split_axis=2, concat_axis=0, tiled=True)
    grad_bias = jnp.transpose(bias_back, (1, 2, 0)).reshape(-1, heads_all)
    grad_in = jnp.dot(
        grad_bias, bias_weight.astype(jnp.float32).T, precision=lax.Precision.HIGHEST
    ).reshape(rows_here, cols_here, channels)
    pair_grad = norm_back(grad_in, updated, bias_gain)
    weight_part = jnp.dot(
        flat_bias.astype(jnp.float32).T, grad_bias, precision=lax.Precision.HIGHEST
    )
    bias_weight_grad = lax.psum(weight_part, ("group", "row", "col"))
    return (
        updated.astype(jnp.bfloat16),
        pair_grad,
        bias_weight_grad,
        denoised,
        token_grad,
        weight_grad,
        out_grad,
    )


def solution(mesh):
    return jax.shard_map(
        shards,
        mesh=mesh,
        in_specs=(
            P(("group", "row"), "col", None),
            P(("group", "row"), "col"),
            P(),
            P(),
            P(),
            P(),
            P(),
            P(),
            P(),
            P(),
            P(),
            P(("group", "row"), None, None),
            P(("group", "row")),
            P(),
            P(None, None, "col"),
            P("col", None),
            P(("group", "row"), None, None),
        ),
        out_specs=(
            P(("group", "row"), "col", None),
            P(("group", "row"), "col", None),
            P(),
            P(("group", "row"), "col", None),
            P(("group", "row"), "col", None),
            P(None, ("group", "row"), "col"),
            P("col", ("group", "row")),
        ),
        check_vma=False,
    )
```

profile of v0, /device:TPU:0, one launch (start us, length us, event | category | flops | bytes accessed | tf_op | source)
XLA Modules:
  0.0 379.4 jit_solution(1215166958934254684)
XLA Ops:
  7.2 1.0 convert_reduce_fusion
  8.3 1.2 fusion.53
  9.5 1.0 copy.117
  11.2 1.1 fusion.55
  12.6 0.8 fusion.76
  14.0 25.8 %all-gather.2.cloned.1.call-done = bf16[128,128,32]{0,2,1:T(8,128)(2,1)} async-done(((bf16[128,16,32]{0,2,1:T(8,128)(2,1)}), bf16[128,128,32]{0,2,1:T(8,128)(2,1)}) %all-gather.2.cloned.1.call-update) | async-done | bytes 1048592 | tf_op jit(solution)/shard_map/all_gather | solution.py:86
  39.7 7.3 %copy.96 = bf16[128,128,32]{2,1,0:T(8,128)(2,1)} copy(bf16[128,128,32]{0,2,1:T(8,128)(2,1)} %all-gather.2.cloned.1.call-done) | data formatting | bytes 2097152 | tf_op jit(solution)/shard_map/all_gather | solution.py:86
  47.0 4.4 %fusion.84 = f32[128,128,16]{1,2,0:T(8,128)S(1)} fusion(bf16[128,128,32]{2,1,0:T(8,128)(2,1)} %copy.96, bf16[128,16,32]{2,1,0:T(8,128)(2,1)S(1)} %copy.97), kind=kOutput, calls=%fused_computation.149 | convolution fusion | flops 16777216 | bytes 2228224 | tf_op jit(solution)/shard_map/cjk,cik->cji/dot_general | solution.py:84
  51.5 1.6 copy.98
  53.6 27.0 %reduce-scatter.8.cloned.1.call-done = f32[128,32,16]{0,2,1:T(8,128)} async-done(((f32[128,128,16]{0,2,1:T(8,128)}), f32[128,32,16]{0,2,1:T(8,128)}) %reduce-scatter.8.cloned.1.call-update) | async-done | bytes 262160 | tf_op jit(solution)/shard_map/reduce_scatter | solution.py:90
  80.5 1.1 bitcast_reduce_fusion
  81.8 1.2 multiply_reduce_fusion.6
  83.1 1.2 multiply_convert_fusion.5
  86.5 3.3 all-to-all-start
  89.8 5.5 %all-to-all-done = bf16[4,2,1024]{2,1,0:T(2,128)(2,1)S(1)} async-done(((bf16[4,2,1024]{2,1,0:T(2,128)(2,1)}), bf16[4,2,1024]{2,1,0:T(2,128)(2,1)S(1)}, u32[]{:S(2)}, u32[]{:S(2)}) %all-to-all-start) | async-done | bytes 16416 | tf_op jit(solution)/shard_map/all_to_all | solution.py:107
  95.6 9.2 %all_gather.7 = bf16[4,128,128]{2,0,1:T(4,128)(2,1)S(1)} all-gather(bf16[4,16,128]{2,0,1:T(4,128)(2,1)S(1)} %all_to_all.29), channel_id=1, replica_groups=mesh['group'=2,'row'=4,'col'=4] {'group','row'}, dimensions={1}, use_global_device_ids=true | all-gather | bytes 147456 | tf_op jit(solution)/shard_map/all_gather | solution.py:108
  105.6 66.1 %while.19 = (s32[]{:T(128)}, f32[4,128,128]{1,2,0:T(8,128)}, f32[4,768,192]{1,2,0:T(8,128)S(1)}, f32[192,768]{1,0:T(8,128)}, bf16[3,128,192]{1,2,0:T(8,128)(2,1)...) while((s32[]{:T(128)}, f32[4,128,128]{1,2,0:T(8,128)}, ...), condition=%wide.region_12.13_spmd.clone, body=%wide.region_7.12_spmd.clone.sunk | while | flops 421316096 | bytes 18337588 | solution.py:195
  107.5 2.4 fusion.165
  110.0 0.9 fusion.167
  110.9 1.9 fusion.168
  112.8 1.9 fusion.169
  115.7 1.8 multiply_reduce_fusion.11
  117.5 1.8 fusion.171
  119.7 1.3 convolution_convert_fusion.2
  121.0 1.5 maximum_dynamic-update-slice_fusion.2
  122.5 2.2 bitcast_add_fusion.2
  124.8 2.0 convolution_add_fusion.2
  129.3 2.4 fusion.165
  131.8 0.9 fusion.167
  132.7 1.9 fusion.168
  134.6 1.9 fusion.169
  137.5 1.8 multiply_reduce_fusion.11
  139.3 1.9 fusion.171
  141.6 1.3 convolution_convert_fusion.2
  142.9 1.5 maximum_dynamic-update-slice_fusion.2
  144.4 2.2 bitcast_add_fusion.2
  146.7 2.2 convolution_add_fusion.2
  151.5 2.4 fusion.165
  153.9 0.9 fusion.167
  154.9 1.9 fusion.168
  156.7 1.9 fusion.169
  159.6 1.8 multiply_reduce_fusion.11
  161.5 1.9 fusion.171
  163.7 1.3 convolution_convert_fusion.2
  165.0 1.5 maximum_dynamic-update-slice_fusion.2
  166.5 2.2 bitcast_add_fusion.2
  168.8 2.2 convolution_add_fusion.2
  171.6 1.8 copy.107
  173.5 2.3 copy.118
  175.9 3.2 convolution_bitcast_fusion
  179.1 2.3 fusion.48
  181.5 2.3 copy.110
  186.1 38.7 %all-reduce.3.cloned.1.call-done = f32[4,128,128]{2,0,1:T(4,128)} async-done(((f32[4,128,128]{2,0,1:T(4,128)}), f32[4,128,128]{2,0,1:T(4,128)}) %all-reduce.3.cloned.1.call-update) | async-done | bytes 262160
  225.8 0.8 reshape.298
  226.6 4.6 %all-to-all-start.1 = ((f32[4,1,2048]{2,1,0:T(1,128)}), f32[4,1,2048]{2,1,0:T(1,128)S(1)}, u32[]{:S(2)}, u32[]{:S(2)}) async-start(f32[4,1,2048]{2,1,0:T(1,128)} %reshape.298), calls=%async_computation.2 | async-start | bytes 65536 | tf_op jit(solution)/shard_map/all_to_all | solution.py:221
  231.2 5.7 %all-to-all-done.1 = f32[4,1,2048]{2,1,0:T(1,128)S(1)} async-done(((f32[4,1,2048]{2,1,0:T(1,128)}), f32[4,1,2048]{2,1,0:T(1,128)S(1)}, u32[]{:S(2)}, u32[]{:S(2)}) %all-to-all-start.1) | async-done | bytes 32800 | tf_op jit(solution)/shard_map/all_to_all | solution.py:221
  238.9 38.5 %psum.7 = f32[128,16]{0,1:T(8,128)} all-reduce(f32[128,16]{0,1:T(8,128)S(1)} %convolution_bitcast_fusion.2), channel_id=1, replica_groups=mesh['group'=2,'row'=4,'col'=4] {'group','row','col'}, use_global_device_ids=true, to_apply=%region_16.17 | all-reduce | flops 2048 | bytes 16384 | tf_op jit(solution)/shard_map/psum | solution.py:230
  277.9 1.0 subtract_multiply_fusion.1
  279.0 1.6 copy.119
  280.6 13.2 %reduce-scatter.12.cloned.1.call-done = f32[3,32,768]{2,1,0:T(8,128)} async-done(((f32[3,128,768]{2,1,0:T(8,128)}), f32[3,32,768]{2,1,0:T(8,128)}) %reduce-scatter.12.cloned.1.call-update) | async-done | bytes 294928 | tf_op jit(solution)/shard_map/reduce_scatter | solution.py:207
  293.8 1.2 multiply_reduce_fusion.7
  295.0 29.0 %reduce-scatter.10.cloned.1.call-done = f32[3,32,768]{2,1,0:T(8,128)} async-done(((f32[3,128,768]{2,1,0:T(8,128)}), f32[3,32,768]{2,1,0:T(8,128)}) %reduce-scatter.10.cloned.1.call-update) | async-done | bytes 294928 | tf_op jit(solution)/shard_map/reduce_scatter | solution.py:206
  323.9 2.0 multiply_convert_fusion.3
  325.9 46.6 %reduce-scatter.14.cloned.1.call-done = f32[4,96,192]{2,1,0:T(8,128)} async-done(((f32[4,768,192]{2,1,0:T(8,128)}), f32[4,96,192]{2,1,0:T(8,128)}) %reduce-scatter.14.cloned.1.call-update) | async-done | bytes 294928 | tf_op jit(solution)/shard_map/reduce_scatter | solution.py:219
  (159 shorter events, 22.9 us)
Async XLA Ops:
  7.2 77.1 %copy-start = (bf16[128,128]{1,0:T(8,128)(2,1)S(1)}, bf16[128,128]{1,0:T(8,128)(2,1)}, u32[]{:S(2)}) copy-start(bf16[128,128]{1,0:T(8,128)(2,1)} %param.26) | copy-start | bytes 98308
  7.2 32.5 %all-gather.2.cloned.1.call-start = ((), (), s32[]{:S(2)}) async-start(), calls=%async_computation.7 | async-start | bytes 1179648 | tf_op jit(solution)/shard_map/all_gather | solution.py:86
  13.5 67.1 %reduce-scatter.8.cloned.1.call-start = ((), (), s32[]{:S(2)}) async-start(), calls=%async_computation.8 | async-start | bytes 1310720 | tf_op jit(solution)/shard_map/reduce_scatter | solution.py:90
  51.4 1.7 copy-start.17
  51.4 1.9 copy-start.16
  51.4 31.7 %copy-start.15 = (f32[128]{0:T(128)S(1)}, f32[128]{0:T(128)}, u32[]{:S(2)}) copy-start(f32[128]{0:T(128)} %param.25) | copy-start | bytes 1540
  51.4 32.9 %copy-start.7 = (bf16[16,32,128]{2,1,0:T(8,128)(2,1)S(1)}, bf16[16,32,128]{2,1,0:T(8,128)(2,1)}, u32[]{:S(2)}) copy-start(bf16[16,32,128]{2,1,0:T(8,128)(2,1)} %param.19) | copy-start | bytes 393220
  53.1 32.3 %copy-start.11 = (bf16[128,16]{0,1:T(8,128)(2,1)S(1)}, bf16[128,16]{0,1:T(8,128)(2,1)}, u32[]{:S(2)}) copy-start(bf16[128,16]{0,1:T(8,128)(2,1)} %param.28) | copy-start | bytes 12292
  53.1 32.3 %copy-start.13 = (f32[128]{0:T(128)S(1)}, f32[128]{0:T(128)}, u32[]{:S(2)}) copy-start(f32[128]{0:T(128)} %param.27) | copy-start | bytes 1540
  53.1 32.3 %copy-start.18 = (f32[16]{0:T(128)S(1)}, f32[16]{0:T(128)}, u32[]{:S(2)}) copy-start(f32[16]{0:T(128)} %param.29) | copy-start | bytes 196
  53.1 36.7 %copy-start.19 = (s32[3]{0:T(128)S(1)}, s32[3]{0:T(128)}, u32[]{:S(2)}) copy-start(s32[3]{0:T(128)} %param.31) | copy-start | bytes 40
  53.3 52.2 %copy-start.1 = (bf16[3,128,768]{2,1,0:T(8,128)(2,1)S(1)}, bf16[3,128,768]{2,1,0:T(8,128)(2,1)}, u32[]{:S(2)}) copy-start(bf16[3,128,768]{2,1,0:T(8,128)(2,1)} %param.30) | copy-start | bytes 1769476
  53.3 52.2 %copy-start.9 = (f32[768]{0:T(1024)S(1)}, f32[768]{0:T(1024)}, u32[]{:S(2)}) copy-start(f32[768]{0:T(1024)} %param.32) | copy-start | bytes 9220
  84.6 0.7 copy-start.5
  86.5 8.8 %all-to-all-start = ((bf16[4,2,1024]{2,1,0:T(2,128)(2,1)}), bf16[4,2,1024]{2,1,0:T(2,128)(2,1)S(1)}, u32[]{:S(2)}, u32[]{:S(2)}) async-start(bf16[4,2,1024]{2,1,0:T(2,128)(2,1)} %reshape.296), calls=%async_computation.1 | async-start | bytes 32768 | tf_op jit(solution)/shard_map/all_to_all | solution.py:107
  89.7 135.1 %all-reduce.3.cloned.1.call-start = ((), (), s32[]{:S(2)}) async-start(), calls=%async_computation.13 | async-start | bytes 524288
  105.6 4.4 %copy-start.4 = (f32[4,128,128]{1,2,0:T(8,128)S(1)}, f32[4,128,128]{1,2,0:T(8,128)}, u32[]{:S(2)}) copy-start(f32[4,128,128]{1,2,0:T(8,128)} %get-tuple-element.359) | copy-start | bytes 786436 | tf_op jit(solution)/shard_map/while
  114.7 2.8 copy-start.8
  115.0 0.7 copy-start.2
  122.5 2.2 copy-start.3
  127.4 4.4 %copy-start.4 = (f32[4,128,128]{1,2,0:T(8,128)S(1)}, f32[4,128,128]{1,2,0:T(8,128)}, u32[]{:S(2)}) copy-start(f32[4,128,128]{1,2,0:T(8,128)} %get-tuple-element.359) | copy-start | bytes 786436 | tf_op jit(solution)/shard_map/while
  136.5 2.8 copy-start.8
  136.8 0.7 copy-start.2
  144.4 2.2 copy-start.3
  149.5 4.4 %copy-start.4 = (f32[4,128,128]{1,2,0:T(8,128)S(1)}, f32[4,128,128]{1,2,0:T(8,128)}, u32[]{:S(2)}) copy-start(f32[4,128,128]{1,2,0:T(8,128)} %get-tuple-element.359) | copy-start | bytes 786436 | tf_op jit(solution)/shard_map/while
  158.7 2.8 copy-start.8
  158.9 0.7 copy-start.2
  166.5 2.2 copy-start.3
  173.5 105.5 %reduce-scatter.16.cloned.1.call-start = ((), (), s32[]{:S(2)}) async-start(), calls=%async_computation.12 | async-start | bytes 884736
  175.8 3.3 copy-start.10
  175.8 118.0 %reduce-scatter.12.cloned.1.call-start = ((), (), s32[]{:S(2)}) async-start(), calls=%async_computation.10 | async-start | bytes 1474560 | tf_op jit(solution)/shard_map/reduce_scatter | solution.py:207
  179.1 144.8 %reduce-scatter.10.cloned.1.call-start = ((), (), s32[]{:S(2)}) async-start(), calls=%async_computation.9 | async-start | bytes 1474560 | tf_op jit(solution)/shard_map/reduce_scatter | solution.py:206
  181.4 191.1 %reduce-scatter.14.cloned.1.call-start = ((), (), s32[]{:S(2)}) async-start(), calls=%async_computation.11 | async-start | bytes 3538944 | tf_op jit(solution)/shard_map/reduce_scatter | solution.py:219
  183.8 0.7 copy-start.20
  183.8 54.7 %copy-start.6 = (f32[16,32,128]{2,1,0:T(8,128)S(1)}, f32[16,32,128]{2,1,0:T(8,128)}, u32[]{:S(2)}) copy-start(f32[16,32,128]{2,1,0:T(8,128)} %copy-done.5) | copy-start | bytes 786436
  183.8 54.7 %copy-start.14 = (f32[128]{0:T(128)S(1)}, f32[128]{0:T(128)}, u32[]{:S(2)}) copy-start(f32[128]{0:T(128)} %param.27) | copy-start | bytes 1540
  183.8 93.5 %copy-start.12 = (bf16[128,16]{0,1:T(8,128)(2,1)S(1)}, bf16[128,16]{0,1:T(8,128)(2,1)}, u32[]{:S(2)}) copy-start(bf16[128,16]{0,1:T(8,128)(2,1)} %param.28) | copy-start | bytes 12292
  226.6 10.3 %all-to-all-start.1 = ((f32[4,1,2048]{2,1,0:T(1,128)}), f32[4,1,2048]{2,1,0:T(1,128)S(1)}, u32[]{:S(2)}, u32[]{:S(2)}) async-start(f32[4,1,2048]{2,1,0:T(1,128)} %reshape.298), calls=%async_computation.2 | async-start | bytes 65536 | tf_op jit(solution)/shard_map/all_to_all | solution.py:221
Sparse Core Ops, SparseCore 0:
  13.6 26.0 all-gather.1
  53.2 27.2 reduce-scatter.7
  173.6 51.1 all-reduce.2
  227.8 34.3 reduce-scatter.15
  264.4 29.3 reduce-scatter.11
  296.0 27.9 reduce-scatter.9
  327.9 44.6 reduce-scatter.13
where the time goes:
time: 381 us; the launch traced here: 379 us
  waiting for transfers between devices  191 us (50%)
  matrix products  52.1 us (14%)
  blocking collectives  47.6 us (12%)
  other arithmetic  33.9 us (9%)
  local copies, waits for them, and re-layouts  30.6 us (8%)
  between operations  15.2 us (4%)
  starting transfers between devices  8.14 us (2%)
    reduce_scatter x1, waiting for transfers between devices, shards(): lax.psum_scatter(weight_sums, ('group', 'row'), scatter_dimension=1, tile...  46.6 us
    unnamed x9, waiting for transfers between devices  38.9 us
    psum x1, blocking collectives, shards(): bias_weight_grad = lax.psum(weight_part, ('group', 'row', 'col'))  38.5 us
    reduce_scatter x1, waiting for transfers between devices, shards(): lax.psum_scatter(attn_parts, 'col', scatter_dimension=1, tiled=True)  29 us
    reduce_scatter x1, waiting for transfers between devices, shards(): lax.psum_scatter(partial_rows, 'col', scatter_dimension=1, tiled=True)  27 us
    all_gather x1, waiting for transfers between devices, shards(): lax.all_gather(right_major, ('group', 'row'), axis=1, tiled=True)  25.8 us
    reduce_scatter x1, waiting for transfers between devices, shards(): lax.psum_scatter(hidden_parts, 'col', scatter_dimension=1, tiled=True)  13.2 us
    all_gather x1, blocking collectives, shards(): lax.all_gather(head_rows, ('group', 'row'), axis=1, tiled=True)  9.18 us
  transfers between devices with their start and end apart: 9, of which 8 were waited for; matrix products, arithmetic and copies ran while one was open for 6% of the time, Pallas kernels for 0%

commit v1 on v0

--- a/solution.py
+++ b/solution.py
@@ -227,7 +227,9 @@
     weight_part = jnp.dot(
         flat_bias.astype(jnp.float32).T, grad_bias, precision=lax.Precision.HIGHEST
     )
-    bias_weight_grad = lax.psum(weight_part, ("group", "row", "col"))
+    bias_weight_grad = weight_part
+    for mesh_axis in (("row", "col"), "group"):
+        bias_weight_grad = lax.psum(bias_weight_grad, mesh_axis)
     return (
         updated.astype(jnp.bfloat16),
         pair_grad,

time: 381 us -> 381 us (level)
    psum x1 -> x2, blocking collectives: 38.5 us -> 36.8 us  [shards(): bias_weight_grad = lax.psum(bias_weight_grad, mesh_axis)]
where the time goes in v1:
time: 381 us; the launch traced here: 379 us
  waiting for transfers between devices  193 us (51%)
  matrix products  52.2 us (14%)
  blocking collectives  46 us (12%)
  other arithmetic  33.9 us (9%)
  local copies, waits for them, and re-layouts  30.6 us (8%)
  between operations  15.2 us (4%)
  starting transfers between devices  8.14 us (2%)
    reduce_scatter x1, waiting for transfers between devices, shards(): lax.psum_scatter(weight_sums, ('group', 'row'), scatter_dimension=1, tile...  46.6 us
    unnamed x9, waiting for transfers between devices  38.9 us
    psum x2, blocking collectives, shards(): bias_weight_grad = lax.psum(bias_weight_grad, mesh_axis)  36.8 us
    reduce_scatter x1, waiting for transfers between devices, shards(): lax.psum_scatter(attn_parts, 'col', scatter_dimension=1, tiled=True)  29 us
    reduce_scatter x1, waiting for transfers between devices, shards(): lax.psum_scatter(partial_rows, 'col', scatter_dimension=1, tiled=True)  27 us
    all_gather x1, waiting for transfers between devices, shards(): lax.all_gather(right_major, ('group', 'row'), axis=1, tiled=True)  25.8 us
    reduce_scatter x1, waiting for transfers between devices, shards(): lax.psum_scatter(hidden_parts, 'col', scatter_dimension=1, tiled=True)  14.8 us
    all_gather x1, blocking collectives, shards(): lax.all_gather(head_rows, ('group', 'row'), axis=1, tiled=True)  9.17 us
  transfers between devices with their start and end apart: 9, of which 8 were waited for; matrix products, arithmetic and copies ran while one was open for 6% of the time, Pallas kernels for 0%

profile of v1, /device:TPU:0, one launch (start us, length us, event | category | flops | bytes accessed | tf_op | source)
XLA Modules:
  0.0 379.4 jit_solution(13662844997040377966)
XLA Ops:
  7.2 1.0 convert_reduce_fusion
  8.3 1.2 fusion.53
  9.5 1.0 copy.117
  11.2 1.1 fusion.55
  14.0 25.8 %all-gather.2.cloned.1.call-done = bf16[128,128,32]{0,2,1:T(8,128)(2,1)} async-done(((bf16[128,16,32]{0,2,1:T(8,128)(2,1)}), bf16[128,128,32]{0,2,1:T(8,128)(2,1)}) %all-gather.2.cloned.1.call-update) | async-done | bytes 1048592 | tf_op jit(solution)/shard_map/all_gather | solution.py:86
  39.7 7.3 %copy.96 = bf16[128,128,32]{2,1,0:T(8,128)(2,1)} copy(bf16[128,128,32]{0,2,1:T(8,128)(2,1)} %all-gather.2.cloned.1.call-done) | data formatting | bytes 2097152 | tf_op jit(solution)/shard_map/all_gather | solution.py:86
  47.0 4.4 %fusion.84 = f32[128,128,16]{1,2,0:T(8,128)S(1)} fusion(bf16[128,128,32]{2,1,0:T(8,128)(2,1)} %copy.96, bf16[128,16,32]{2,1,0:T(8,128)(2,1)S(1)} %copy.97), kind=kOutput, calls=%fused_computation.149 | convolution fusion | flops 16777216 | bytes 2228224 | tf_op jit(solution)/shard_map/cjk,cik->cji/dot_general | solution.py:84
  51.5 1.6 copy.98
  53.6 27.0 %reduce-scatter.8.cloned.1.call-done = f32[128,32,16]{0,2,1:T(8,128)} async-done(((f32[128,128,16]{0,2,1:T(8,128)}), f32[128,32,16]{0,2,1:T(8,128)}) %reduce-scatter.8.cloned.1.call-update) | async-done | bytes 262160 | tf_op jit(solution)/shard_map/reduce_scatter | solution.py:90
  80.5 1.1 bitcast_reduce_fusion
  81.8 1.2 multiply_reduce_fusion.6
  83.1 1.2 multiply_convert_fusion.5
  86.5 3.3 all-to-all-start
  89.8 5.5 %all-to-all-done = bf16[4,2,1024]{2,1,0:T(2,128)(2,1)S(1)} async-done(((bf16[4,2,1024]{2,1,0:T(2,128)(2,1)}), bf16[4,2,1024]{2,1,0:T(2,128)(2,1)S(1)}, u32[]{:S(2)}, u32[]{:S(2)}) %all-to-all-start) | async-done | bytes 16416 | tf_op jit(solution)/shard_map/all_to_all | solution.py:107
  95.6 9.2 %all_gather.7 = bf16[4,128,128]{2,0,1:T(4,128)(2,1)S(1)} all-gather(bf16[4,16,128]{2,0,1:T(4,128)(2,1)S(1)} %all_to_all.29), channel_id=1, replica_groups=mesh['group'=2,'row'=4,'col'=4] {'group','row'}, dimensions={1}, use_global_device_ids=true | all-gather | bytes 147456 | tf_op jit(solution)/shard_map/all_gather | solution.py:108
  105.6 66.1 %while.19 = (s32[]{:T(128)}, f32[4,128,128]{1,2,0:T(8,128)}, f32[4,768,192]{1,2,0:T(8,128)S(1)}, f32[192,768]{1,0:T(8,128)}, bf16[3,128,192]{1,2,0:T(8,128)(2,1)...) while((s32[]{:T(128)}, f32[4,128,128]{1,2,0:T(8,128)}, ...), condition=%wide.region_12.13_spmd.clone, body=%wide.region_7.12_spmd.clone.sunk | while | flops 421316096 | bytes 18337588 | solution.py:195
  107.5 2.4 fusion.165
  110.0 0.9 fusion.167
  110.9 1.9 fusion.168
  112.8 1.9 fusion.169
  115.7 1.8 multiply_reduce_fusion.11
  117.5 1.8 fusion.171
  119.7 1.3 convolution_convert_fusion.2
  121.0 1.5 maximum_dynamic-update-slice_fusion.2
  122.5 2.2 bitcast_add_fusion.2
  124.8 2.0 convolution_add_fusion.2
  129.4 2.4 fusion.165
  131.8 0.9 fusion.167
  132.7 1.9 fusion.168
  134.6 1.9 fusion.169
  137.5 1.8 multiply_reduce_fusion.11
  139.3 1.9 fusion.171
  141.6 1.3 convolution_convert_fusion.2
  142.9 1.5 maximum_dynamic-update-slice_fusion.2
  144.4 2.2 bitcast_add_fusion.2
  146.7 2.2 convolution_add_fusion.2
  151.5 2.4 fusion.165
  153.9 0.9 fusion.167
  154.9 1.9 fusion.168
  156.7 1.9 fusion.169
  159.6 1.8 multiply_reduce_fusion.11
  161.5 1.9 fusion.171
  163.7 1.3 convolution_convert_fusion.2
  165.0 1.5 maximum_dynamic-update-slice_fusion.2
  166.5 2.2 bitcast_add_fusion.2
  168.8 2.2 convolution_add_fusion.2
  171.6 1.8 copy.107
  173.5 2.3 copy.118
  175.9 3.2 convolution_bitcast_fusion
  179.1 2.3 fusion.48
  181.5 2.3 copy.110
  186.1 38.7 %all-reduce.3.cloned.1.call-done = f32[4,128,128]{2,0,1:T(4,128)} async-done(((f32[4,128,128]{2,0,1:T(4,128)}), f32[4,128,128]{2,0,1:T(4,128)}) %all-reduce.3.cloned.1.call-update) | async-done | bytes 262160
  225.8 0.8 reshape.298
  226.6 4.6 %all-to-all-start.1 = ((f32[4,1,2048]{2,1,0:T(1,128)}), f32[4,1,2048]{2,1,0:T(1,128)S(1)}, u32[]{:S(2)}, u32[]{:S(2)}) async-start(f32[4,1,2048]{2,1,0:T(1,128)} %reshape.298), calls=%async_computation.2 | async-start | bytes 65536 | tf_op jit(solution)/shard_map/all_to_all | solution.py:221
  231.2 5.7 %all-to-all-done.1 = f32[4,1,2048]{2,1,0:T(1,128)S(1)} async-done(((f32[4,1,2048]{2,1,0:T(1,128)}), f32[4,1,2048]{2,1,0:T(1,128)S(1)}, u32[]{:S(2)}, u32[]{:S(2)}) %all-to-all-start.1) | async-done | bytes 32800 | tf_op jit(solution)/shard_map/all_to_all | solution.py:221
  238.9 31.2 %psum.14 = f32[128,16]{0,1:T(8,128)S(1)} all-reduce(f32[128,16]{0,1:T(8,128)S(1)} %convolution_bitcast_fusion.2), channel_id=1, replica_groups=mesh['group'=2,'row'=4,'col'=4] {'row','col'}, use_global_device_ids=true, to_apply=%region_16.17 | all-reduce | flops 2048 | bytes 16384 | tf_op jit(solution)/shard_map/psum | solution.py:232
  270.1 5.6 %psum.15 = f32[128,16]{0,1:T(8,128)} all-reduce(f32[128,16]{0,1:T(8,128)S(1)} %psum.14), channel_id=1, replica_groups=mesh['group'=2,'row'=4,'col'=4] {'group'}, use_global_device_ids=true, to_apply=%region_17.18 | all-reduce | flops 2048 | bytes 16384 | tf_op jit(solution)/shard_map/psum | solution.py:232
  276.3 1.0 subtract_multiply_fusion.1
  277.3 1.6 copy.119
  279.0 14.8 %reduce-scatter.12.cloned.1.call-done = f32[3,32,768]{2,1,0:T(8,128)} async-done(((f32[3,128,768]{2,1,0:T(8,128)}), f32[3,32,768]{2,1,0:T(8,128)}) %reduce-scatter.12.cloned.1.call-update) | async-done | bytes 294928 | tf_op jit(solution)/shard_map/reduce_scatter | solution.py:207
  293.8 1.2 multiply_reduce_fusion.7
  295.0 29.0 %reduce-scatter.10.cloned.1.call-done = f32[3,32,768]{2,1,0:T(8,128)} async-done(((f32[3,128,768]{2,1,0:T(8,128)}), f32[3,32,768]{2,1,0:T(8,128)}) %reduce-scatter.10.cloned.1.call-update) | async-done | bytes 294928 | tf_op jit(solution)/shard_map/reduce_scatter | solution.py:206
  323.9 2.0 multiply_convert_fusion.3
  326.0 46.6 %reduce-scatter.14.cloned.1.call-done = f32[4,96,192]{2,1,0:T(8,128)} async-done(((f32[4,768,192]{2,1,0:T(8,128)}), f32[4,96,192]{2,1,0:T(8,128)}) %reduce-scatter.14.cloned.1.call-update) | async-done | bytes 294928 | tf_op jit(solution)/shard_map/reduce_scatter | solution.py:219
  (160 shorter events, 23.8 us)
Async XLA Ops:
  7.2 77.1 %copy-start = (bf16[128,128]{1,0:T(8,128)(2,1)S(1)}, bf16[128,128]{1,0:T(8,128)(2,1)}, u32[]{:S(2)}) copy-start(bf16[128,128]{1,0:T(8,128)(2,1)} %param.26) | copy-start | bytes 98308
  7.2 32.5 %all-gather.2.cloned.1.call-start = ((), (), s32[]{:S(2)}) async-start(), calls=%async_computation.7 | async-start | bytes 1179648 | tf_op jit(solution)/shard_map/all_gather | solution.py:86
  13.5 67.1 %reduce-scatter.8.cloned.1.call-start = ((), (), s32[]{:S(2)}) async-start(), calls=%async_computation.8 | async-start | bytes 1310720 | tf_op jit(solution)/shard_map/reduce_scatter | solution.py:90
  51.4 1.7 copy-start.17
  51.4 1.9 copy-start.16
  51.4 31.7 %copy-start.15 = (f32[128]{0:T(128)S(1)}, f32[128]{0:T(128)}, u32[]{:S(2)}) copy-start(f32[128]{0:T(128)} %param.25) | copy-start | bytes 1540
  51.4 32.9 %copy-start.7 = (bf16[16,32,128]{2,1,0:T(8,128)(2,1)S(1)}, bf16[16,32,128]{2,1,0:T(8,128)(2,1)}, u32[]{:S(2)}) copy-start(bf16[16,32,128]{2,1,0:T(8,128)(2,1)} %param.19) | copy-start | bytes 393220
  53.1 32.3 %copy-start.11 = (bf16[128,16]{0,1:T(8,128)(2,1)S(1)}, bf16[128,16]{0,1:T(8,128)(2,1)}, u32[]{:S(2)}) copy-start(bf16[128,16]{0,1:T(8,128)(2,1)} %param.28) | copy-start | bytes 12292
  53.1 32.3 %copy-start.13 = (f32[128]{0:T(128)S(1)}, f32[128]{0:T(128)}, u32[]{:S(2)}) copy-start(f32[128]{0:T(128)} %param.27) | copy-start | bytes 1540
  53.1 32.3 %copy-start.18 = (f32[16]{0:T(128)S(1)}, f32[16]{0:T(128)}, u32[]{:S(2)}) copy-start(f32[16]{0:T(128)} %param.29) | copy-start | bytes 196
  53.1 36.7 %copy-start.19 = (s32[3]{0:T(128)S(1)}, s32[3]{0:T(128)}, u32[]{:S(2)}) copy-start(s32[3]{0:T(128)} %param.31) | copy-start | bytes 40
  53.3 52.2 %copy-start.1 = (bf16[3,128,768]{2,1,0:T(8,128)(2,1)S(1)}, bf16[3,128,768]{2,1,0:T(8,128)(2,1)}, u32[]{:S(2)}) copy-start(bf16[3,128,768]{2,1,0:T(8,128)(2,1)} %param.30) | copy-start | bytes 1769476
  53.3 52.2 %copy-start.9 = (f32[768]{0:T(1024)S(1)}, f32[768]{0:T(1024)}, u32[]{:S(2)}) copy-start(f32[768]{0:T(1024)} %param.32) | copy-start | bytes 9220
  84.6 0.7 copy-start.5
  86.5 8.8 %all-to-all-start = ((bf16[4,2,1024]{2,1,0:T(2,128)(2,1)}), bf16[4,2,1024]{2,1,0:T(2,128)(2,1)S(1)}, u32[]{:S(2)}, u32[]{:S(2)}) async-start(bf16[4,2,1024]{2,1,0:T(2,128)(2,1)} %reshape.296), calls=%async_computation.1 | async-start | bytes 32768 | tf_op jit(solution)/shard_map/all_to_all | solution.py:107
  89.7 135.1 %all-reduce.3.cloned.1.call-start = ((), (), s32[]{:S(2)}) async-start(), calls=%async_computation.13 | async-start | bytes 524288
  105.6 4.4 %copy-start.4 = (f32[4,128,128]{1,2,0:T(8,128)S(1)}, f32[4,128,128]{1,2,0:T(8,128)}, u32[]{:S(2)}) copy-start(f32[4,128,128]{1,2,0:T(8,128)} %get-tuple-element.359) | copy-start | bytes 786436 | tf_op jit(solution)/shard_map/while
  114.7 2.8 copy-start.8
  115.0 0.7 copy-start.2
  122.5 2.2 copy-start.3
  127.4 4.4 %copy-start.4 = (f32[4,128,128]{1,2,0:T(8,128)S(1)}, f32[4,128,128]{1,2,0:T(8,128)}, u32[]{:S(2)}) copy-start(f32[4,128,128]{1,2,0:T(8,128)} %get-tuple-element.359) | copy-start | bytes 786436 | tf_op jit(solution)/shard_map/while
  136.5 2.8 copy-start.8
  136.8 0.7 copy-start.2
  144.4 2.2 copy-start.3
  149.5 4.4 %copy-start.4 = (f32[4,128,128]{1,2,0:T(8,128)S(1)}, f32[4,128,128]{1,2,0:T(8,128)}, u32[]{:S(2)}) copy-start(f32[4,128,128]{1,2,0:T(8,128)} %get-tuple-element.359) | copy-start | bytes 786436 | tf_op jit(solution)/shard_map/while
  158.7 2.8 copy-start.8
  158.9 0.7 copy-start.2
  166.5 2.2 copy-start.3
  173.5 103.9 %reduce-scatter.16.cloned.1.call-start = ((), (), s32[]{:S(2)}) async-start(), calls=%async_computation.12 | async-start | bytes 884736
  175.8 3.3 copy-start.10
  175.8 118.0 %reduce-scatter.12.cloned.1.call-start = ((), (), s32[]{:S(2)}) async-start(), calls=%async_computation.10 | async-start | bytes 1474560 | tf_op jit(solution)/shard_map/reduce_scatter | solution.py:207
  179.1 144.9 %reduce-scatter.10.cloned.1.call-start = ((), (), s32[]{:S(2)}) async-start(), calls=%async_computation.9 | async-start | bytes 1474560 | tf_op jit(solution)/shard_map/reduce_scatter | solution.py:206
  181.5 191.1 %reduce-scatter.14.cloned.1.call-start = ((), (), s32[]{:S(2)}) async-start(), calls=%async_computation.11 | async-start | bytes 3538944 | tf_op jit(solution)/shard_map/reduce_scatter | solution.py:219
  183.8 0.7 copy-start.20
  183.8 54.7 %copy-start.6 = (f32[16,32,128]{2,1,0:T(8,128)S(1)}, f32[16,32,128]{2,1,0:T(8,128)}, u32[]{:S(2)}) copy-start(f32[16,32,128]{2,1,0:T(8,128)} %copy-done.5) | copy-start | bytes 786436
  183.8 54.7 %copy-start.14 = (f32[128]{0:T(128)S(1)}, f32[128]{0:T(128)}, u32[]{:S(2)}) copy-start(f32[128]{0:T(128)} %param.27) | copy-start | bytes 1540
  183.8 91.9 %copy-start.12 = (bf16[128,16]{0,1:T(8,128)(2,1)S(1)}, bf16[128,16]{0,1:T(8,128)(2,1)}, u32[]{:S(2)}) copy-start(bf16[128,16]{0,1:T(8,128)(2,1)} %param.28) | copy-start | bytes 12292
  226.6 10.3 %all-to-all-start.1 = ((f32[4,1,2048]{2,1,0:T(1,128)}), f32[4,1,2048]{2,1,0:T(1,128)S(1)}, u32[]{:S(2)}, u32[]{:S(2)}) async-start(f32[4,1,2048]{2,1,0:T(1,128)} %reshape.298), calls=%async_computation.2 | async-start | bytes 65536 | tf_op jit(solution)/shard_map/all_to_all | solution.py:221
Sparse Core Ops, SparseCore 0:
  13.6 26.0 all-gather.1
  53.2 27.2 reduce-scatter.7
  173.6 51.1 all-reduce.2
  227.8 34.4 reduce-scatter.15
  264.5 29.2 reduce-scatter.11
  296.0 27.9 reduce-scatter.9
  327.9 44.6 reduce-scatter.13
